TPU v7x, 512 devices: a whole 4x8x8 slice. The times are simulated.
512 devices in a mesh: seq: 8 (over z), head: 4 (over x_hi, core), ctx: 16 (over y, x_lo).
Axes of the slice: x: 4 (x_hi: 2, x_lo: 2; x = x_hi * 2 + x_lo), y: 8, z: 8, core: 2. Of those that a mesh axis runs over, the one named last changes fastest.
Arguments:
- q_new: bfloat16 [4096, 8192], P('seq', ('head', 'ctx')), may hold values from -6 to 6
- k_prefix: bfloat16 [4096, 1024], P('seq', 'head'), may hold values from -204 to 204
- v_prefix: bfloat16 [4096, 1024], P('seq', 'head'), may hold values from -6 to 6
- k_new: bfloat16 [4096, 1024], P('seq', 'head'), may hold values from -204 to 204
- v_new: bfloat16 [4096, 1024], P('seq', 'head'), may hold values from -6 to 6
- block_offsets: int32 [32], P('seq'), may hold values from 0 to 2047
- dec_hidden: bfloat16 [256, 8192], P(None, 'ctx'), may hold values from -6 to 6
- w_query: bfloat16 [8192, 4, 2048], P('ctx', 'head', 'seq'), may hold values from -0.0625 to 0.0625
- w_out: bfloat16 [4, 2048, 8192], P('head', 'seq', 'ctx'), may hold values from -0.0625 to 0.0625
- k_own: bfloat16 [256, 1024], P(None, 'head'), may hold values from -21 to 21
- v_own: bfloat16 [256, 1024], P(None, 'head'), may hold values from -6 to 6
- valid_len: int32 [256], replicated, may hold values from 1 to 4096
- parent: int32 [256], replicated, may hold values from 0 to 4095
Outputs:
- prefill_out: bfloat16 [4096, 8192], P('seq', ('head', 'ctx'))
- decoded: bfloat16 [256, 8192], P(('seq', 'head'), 'ctx')
All inputs are finite; a program needn't handle non-finite values.
Results may differ from a plain program's by a relative error of at most 0.017.
The roundings to bfloat16 on the way count: a program that leaves them out, or rounds other values in their place, can miss the bound.
Values may be sent and summed in bfloat16 or wider, within the bound.
No kernel may reach another device: no remote copies, remote signals or barrier semaphores. Data moves between devices by JAX's collectives and lax.ppermute only.
A program may use at most 64 MiB of HBM per device.

v0:
```python
import math

import jax
import jax.numpy as jnp
from jax import lax
from jax.sharding import Mesh
from jax.sharding import PartitionSpec as P

HQ = 64
KVH = 8
HD = 128
QBLK = 128
CTX = ("ctx_0", "ctx_1")
HEAD_CTX = ("head", "ctx_0", "ctx_1")


NEG_FILL = -1e30


def side_by_side(arrays, axis, dim, along):
    widths = [a.shape[along] for a in arrays]
    both = jnp.concatenate(arrays, axis=along)
    out = lax.all_gather(both, axis, axis=dim, tiled=True)
    return tuple(jnp.split(out, [sum(widths[:k]) for k in range(1, len(widths))], axis=along))


def sent_to_all(shard, axis):
    devices = lax.axis_size(axis)
    return lax.all_to_all(
        jnp.broadcast_to(shard[None], (devices, *shard.shape)), axis, 0, 0, tiled=True
    )


def of_everyone(shard, axis):
    everything = sent_to_all(shard, axis)
    return jnp.sum(everything, axis=0)


def broadcast(shard, axis, root):
    return lax.dynamic_index_in_dim(lax.all_gather(shard, axis), root, 0, keepdims=False)


def collected_together(shard, axis):
    leaves = jax.tree.leaves(shard)
    order = sorted(range(len(leaves)), key=lambda k: -leaves[k].size)
    width = (1, *leaves[order[0]].shape)[-1]
    lines = [
        jnp.pad(leaves[k].reshape(-1), (0, -leaves[k].size % width)).reshape(-1, width)
        for k in order
    ]
    both, at, found = (lax.all_gather(jnp.concatenate(lines), axis), 0, {})
    for k, line in zip(order, lines):
        piece = both[:, at : at + len(line)].reshape(len(both), -1)
        found[k] = piece[:, : leaves[k].size].reshape(-1, *leaves[k].shape)
        at += len(line)
    numbers = iter(range(len(leaves)))
    return jax.tree.map(lambda _: found[next(numbers)], shard)


def joined_all(shard, axes, combine):
    for axis in axes:
        pieces = collected_together(shard, axis)
        shard = jax.tree.map(lambda part: part[0], pieces)
        for k in range(1, lax.axis_size(axis)):
            shard = combine(shard, jax.tree.map(lambda part: part[k], pieces))
    return shard


def cut_along(shard, dim, devices):
    shape = shard.shape
    tiles = shard.reshape(*shape[:dim], devices, shape[dim] // devices, *shape[dim + 1 :])
    return jnp.moveaxis(tiles, dim, 0)


def sum_at_owner(shard, axis, dim):
    devices = lax.axis_size(axis)
    tiles = lax.all_to_all(cut_along(shard, dim, devices), axis, 0, 0, tiled=True)
    return jnp.sum(tiles.astype(jnp.float32), axis=0)


def online_update(carry, queries, keys, values, visible, scale):
    best, total, accum = carry
    scores = jnp.einsum("qd,kd->qk", queries, keys, preferred_element_type=jnp.float32) * scale
    scores = jnp.where(visible, scores, NEG_FILL)
    fresh = jnp.maximum(best, jnp.max(scores, axis=1))
    factor = jnp.exp(best - fresh)
    weights = jnp.where(visible, jnp.exp(scores - fresh[:, None]), 0.0)
    total = total * factor + jnp.sum(weights, axis=1)
    accum = accum * factor[:, None] + jnp.dot(
        weights.astype(jnp.bfloat16), values, preferred_element_type=jnp.float32
    )
    return (fresh, total, accum)


def combine_parts(left, right):
    best = jnp.maximum(left[0], right[0])
    left_f = jnp.exp(left[0] - best)
    right_f = jnp.exp(right[0] - best)
    return (
        best,
        left[1] * left_f + right[1] * right_f,
        left[2] * left_f[:, None] + right[2] * right_f[:, None],
    )


def body(
    q_new,
    k_prefix,
    v_prefix,
    k_new,
    v_new,
    block_offsets,
    dec_hidden,
    w_query,
    w_out,
    k_own,
    v_own,
    valid_len,
    parent,
):
    group_size = HQ // KVH
    scale = 1.0 / math.sqrt(HD)
    n_seq = lax.axis_size("seq")
    seq_idx = lax.axis_index("seq")
    ctx_idx = lax.axis_index(CTX)
    block = q_new.shape[0]
    per_dev = q_new.shape[1] // HD
    prefix_len = block * n_seq
    kv_pre = ctx_idx * per_dev // group_size
    first_rows = jnp.repeat(block_offsets, QBLK * per_dev)
    qpos_rows = seq_idx * block + jnp.arange(block * per_dev, dtype=jnp.int32) // per_dev

    def head_cols(arr, which):
        return lax.dynamic_slice_in_dim(arr, which * HD, HD, arr.ndim - 1)

    init = (
        jnp.full((block * per_dev,), NEG_FILL, jnp.float32),
        jnp.zeros((block * per_dev,), jnp.float32),
        jnp.zeros((block * per_dev, HD), jnp.float32),
    )
    spans = (
        head_cols(k_prefix, kv_pre),
        head_cols(v_prefix, kv_pre),
        head_cols(k_new, kv_pre),
        head_cols(v_new, kv_pre),
    )
    carry = init
    kp, vp, kn, vn = side_by_side((spans[0], spans[1], spans[2], spans[3]), "seq", 0, 1)
    rows = kp.shape[0]
    step_len = math.gcd(rows, 512)
    count = rows // step_len

    def one(state, items):
        kpb, vpb, knb, vnb, base = items
        pos = base + jnp.arange(step_len, dtype=jnp.int32)
        state = online_update(state, q_new, kpb, vpb, pos[None, :] >= first_rows[:, None], scale)
        state = online_update(state, q_new, knb, vnb, pos[None, :] <= qpos_rows[:, None], scale)
        return (state, None)

    bases = step_len * jnp.arange(count, dtype=jnp.int32)
    carry, _ = lax.scan(
        one,
        carry,
        (
            kp.reshape(count, step_len, HD),
            vp.reshape(count, step_len, HD),
            kn.reshape(count, step_len, HD),
            vn.reshape(count, step_len, HD),
            bases,
        ),
    )
    best, total, accum = carry
    prefill_out = (accum / total[:, None]).astype(jnp.bfloat16)
    partial_q = jnp.dot(
        dec_hidden, w_query.reshape(w_query.shape[0], -1), preferred_element_type=jnp.float32
    )
    dec_q = of_everyone(partial_q, CTX).astype(jnp.bfloat16)
    rows = dec_hidden.shape[0]
    heads_dec = dec_q.shape[1] // HD
    kv_dec = seq_idx * heads_dec // group_size
    source = ctx_idx % n_seq
    mine = jnp.where(ctx_idx >= n_seq, jnp.stack([k_new, v_new]), jnp.stack([k_prefix, v_prefix]))
    span = broadcast(mine, "seq", source)
    span_k = head_cols(span[0], kv_dec)
    span_v = head_cols(span[1], kv_dec)
    dq_rows = dec_q.reshape(rows * heads_dec, HD)
    cache_pos = ctx_idx * block + jnp.arange(block, dtype=jnp.int32)
    length_rows = jnp.repeat(valid_len, heads_dec)
    parent_rows = jnp.repeat(parent, heads_dec)
    visible = jnp.where(
        cache_pos[None, :] < prefix_len,
        cache_pos[None, :] < length_rows[:, None],
        cache_pos[None, :] - prefix_len <= parent_rows[:, None],
    )
    start_state = (
        jnp.full((rows * heads_dec,), NEG_FILL, jnp.float32),
        jnp.zeros((rows * heads_dec,), jnp.float32),
        jnp.zeros((rows * heads_dec, HD), jnp.float32),
    )
    local = online_update(start_state, dq_rows, span_k, span_v, visible, scale)
    best, total, accum = joined_all(local, CTX, combine_parts)
    own_keys = jnp.broadcast_to(
        head_cols(k_own, kv_dec)[:, None, :], (rows, heads_dec, HD)
    ).reshape(rows * heads_dec, HD)
    own_vals = jnp.broadcast_to(
        head_cols(v_own, kv_dec)[:, None, :], (rows, heads_dec, HD)
    ).reshape(rows * heads_dec, HD)
    own_score = jnp.sum(dq_rows.astype(jnp.float32) * own_keys.astype(jnp.float32), axis=1) * scale
    top = jnp.maximum(best, own_score)
    factor = jnp.exp(best - top)
    own_w = jnp.exp(own_score - top)
    own_r = lax.optimization_barrier(own_w.astype(jnp.bfloat16)).astype(jnp.float32)
    total = total * factor + own_w
    accum = accum * factor[:, None] + own_r[:, None] * own_vals.astype(jnp.float32)
    attn = (accum / total[:, None]).astype(jnp.bfloat16).reshape(rows, heads_dec * HD)
    out_weight = w_out.reshape(-1, w_out.shape[2])
    decoded = sum_at_owner(
        jnp.dot(attn, out_weight, preferred_element_type=jnp.float32).astype(jnp.bfloat16),
        ("seq", "head"),
        0,
    ).astype(jnp.bfloat16)
    return (prefill_out, decoded)


def solution(mesh):
    split = Mesh(
        mesh.devices.reshape(mesh.shape["seq"], mesh.shape["head"], 8, 2),
        ("seq", "head", "ctx_0", "ctx_1"),
    )
    return jax.shard_map(
        body,
        mesh=split,
        in_specs=(
            P("seq", HEAD_CTX),
            P("seq", "head"),
            P("seq", "head"),
            P("seq", "head"),
            P("seq", "head"),
            P("seq"),
            P(None, CTX),
            P(CTX, "head", "seq"),
            P("head", "seq", CTX),
            P(None, "head"),
            P(None, "head"),
            P(),
            P(),
        ),
        out_specs=(P("seq", HEAD_CTX), P(("seq", "head"), CTX)),
        check_vma=False,
    )
```

profile of v0, /device:TPU:1, one launch (start us, length us, event | category | flops | bytes accessed | tf_op | source)
XLA Modules:
  0.0 268.8 jit_solution(10456112699704648559)
XLA Ops:
  7.2 2.1 maximum_select_fusion
  9.4 1.3 fusion.74
  10.6 2.3 broadcast_in_dim.46
  13.0 8.9 %all-to-all-start = ((f32[16,256,256]{2,1,0:T(8,128)}), f32[16,256,256]{2,1,0:T(8,128)}, u32[]{:S(2)}, u32[]{:S(2)}) async-start(f32[16,256,256]{2,1,0:T(8,128)} %broadcast_in_dim.46), calls=%async_computation | async-start | bytes 8388608 | tf_op jit(solution)/shard_map/all_to_all | solution.py:29
  23.6 94.3 %all-to-all-done = f32[16,256,256]{2,1,0:T(8,128)} async-done(((f32[16,256,256]{2,1,0:T(8,128)}), f32[16,256,256]{2,1,0:T(8,128)}, u32[]{:S(2)}, u32[]{:S(2)}) %all-to-all-start) | async-done | bytes 4194336 | tf_op jit(solution)/shard_map/all_to_all | solution.py:29
  117.9 2.5 reduce_sum.59
  120.5 1.4 fusion.144
  122.4 1.6 convolution_add_fusion.2
  124.8 7.1 %all-gather.6.cloned.1.call-done = bf16[4096,512]{1,0:T(8,128)(2,1)} async-done(((bf16[512,512]{1,0:T(8,128)(2,1)}), bf16[4096,512]{1,0:T(8,128)(2,1)}) %all-gather.6.cloned.1.call-update) | async-done | bytes 4194320 | tf_op jit(solution)/shard_map/all_gather | solution.py:23
  132.0 4.0 %fusion.141 = (bf16[4096,128]{1,0:T(8,128)(2,1)S(1)}, bf16[4096,128]{1,0:T(8,128)(2,1)}, bf16[4096,128]{1,0:T(8,128)(2,1)}, bf16[4096,128]{1,0:T(8,128)(2,1)}) fusion(bf16[4096,512]{1,0:T(8,128)(2,1)} %all-gather.6.cloned.1.call-done), kind=kLoop, calls=%fused_computation.232 | loop fusion | bytes 8388608 | tf_op jit(solution)/shard_map/split | solution.py:24
  136.2 35.2 %all-gather.10.cloned.1.call-done = f32[4160,128]{1,0:T(8,128)} async-done(((f32[520,128]{1,0:T(8,128)}), f32[4160,128]{1,0:T(8,128)}) %all-gather.10.cloned.1.call-update) | async-done | bytes 2129936 | tf_op jit(solution)/shard_map/all_gather | solution.py:51
  175.1 2.5 fusion.53
  177.6 5.9 %all-gather.1 = f32[1040,128]{1,0:T(8,128)S(1)} all-gather(f32[520,128]{1,0:T(8,128)S(1)} %pad_maximum_fusion.2), channel_id=3, replica_groups=mesh['seq'=8,'head'=4,'ctx_0'=8,'ctx_1'=2] {'ctx_1'}, dimensions={0}, use_global_device_ids=true | all-gather | bytes 798720 | tf_op jit(solution)/shard_map/all_gather | solution.py:51
  184.6 1.7 fusion.76
  187.2 16.1 %all-to-all-start.1 = ((bf16[32,8,512]{2,1,0:T(8,128)(2,1)}), bf16[32,8,512]{2,1,0:T(8,128)(2,1)}, u32[]{:S(2)}, u32[]{:S(2)}) async-start(bf16[32,8,512]{2,1,0:T(8,128)(2,1)} %fusion.41), calls=%async_computation.1 | async-start | bytes 524288 | tf_op jit(solution)/shard_map/all_to_all | solution.py:77
  203.3 55.7 %while.15 = (s32[]{:T(128)}, f32[512]{0:T(512)S(1)}, f32[512]{0:T(512)S(1)}, f32[512,128]{1,0:T(8,128)}, s32[8]{0:T(128)S(1)}, /*index=5*/bf16[8,512,128]{2,1,0:...) while((s32[]{:T(128)}, f32[512]{0:T(512)S(1)}, ...), condition=%wide.region_5.6_spmd.clone, body=%wide.region_0.5_spmd.clone.sunk | while | flops 275059200 | bytes 8208589 | solution.py:161
  204.5 1.3 fusion.168
  205.8 1.3 fusion.167
  207.6 1.4 fusion.172
  211.4 1.3 fusion.168
  212.7 1.3 fusion.167
  214.5 1.5 fusion.172
  216.0 1.1 convolution_add_fusion.4
  218.4 1.3 fusion.168
  219.7 1.3 fusion.167
  221.4 1.5 fusion.172
  222.9 1.1 convolution_add_fusion.4
  225.3 1.3 fusion.168
  226.6 1.3 fusion.167
  228.4 1.5 fusion.172
  229.9 1.1 convolution_add_fusion.4
  232.3 1.3 fusion.168
  233.6 1.3 fusion.167
  235.4 1.5 fusion.172
  236.9 1.1 convolution_add_fusion.4
  239.3 1.3 fusion.168
  240.6 1.3 fusion.167
  242.4 1.5 fusion.172
  243.9 1.1 convolution_add_fusion.4
  246.2 1.3 fusion.168
  247.5 1.3 fusion.167
  249.3 1.5 fusion.172
  250.8 1.1 convolution_add_fusion.4
  253.2 1.3 fusion.168
  254.5 1.3 fusion.167
  256.3 1.5 fusion.172
  259.0 1.7 divide_convert_fusion
  260.7 1.6 reduce_sum.63
  (125 shorter events, 24.8 us)
Async XLA Ops:
  7.2 179.1 %copy-start = (bf16[1,256,512]{2,1,0:T(8,128)(2,1)S(1)}, bf16[1,256,512]{2,1,0:T(8,128)(2,1)}, u32[]{:S(2)}) copy-start(bf16[1,256,512]{2,1,0:T(8,128)(2,1)} %param.23) | copy-start | bytes 786436
  7.2 113.3 %all-gather.8.cloned.1.call-start = ((), (), s32[]{:S(2)}) async-start(), calls=%async_computation.3 | async-start | bytes 4718592 | tf_op jit(solution)/shard_map/all_gather | solution.py:40
  13.0 9.0 %copy-start.1 = (bf16[512,256]{1,0:T(8,128)(2,1)S(1)}, bf16[512,256]{1,0:T(8,128)(2,1)}, u32[]{:S(2)}) copy-start(bf16[512,256]{1,0:T(8,128)(2,1)} %param.19) | copy-start | bytes 786436
  13.0 9.0 %copy-start.2 = (bf16[512,256]{1,0:T(8,128)(2,1)S(1)}, bf16[512,256]{1,0:T(8,128)(2,1)}, u32[]{:S(2)}) copy-start(bf16[512,256]{1,0:T(8,128)(2,1)} %param.18) | copy-start | bytes 786436
  13.0 9.0 %copy-start.3 = (bf16[512,256]{1,0:T(8,128)(2,1)S(1)}, bf16[512,256]{1,0:T(8,128)(2,1)}, u32[]{:S(2)}) copy-start(bf16[512,256]{1,0:T(8,128)(2,1)} %param.17) | copy-start | bytes 786436
  13.0 9.0 %copy-start.4 = (bf16[512,256]{1,0:T(8,128)(2,1)S(1)}, bf16[512,256]{1,0:T(8,128)(2,1)}, u32[]{:S(2)}) copy-start(bf16[512,256]{1,0:T(8,128)(2,1)} %param.16) | copy-start | bytes 786436
  13.0 10.1 %copy-start.8 = (s32[256]{0:T(256)S(1)}, s32[256]{0:T(256)}, u32[]{:S(2)}) copy-start(s32[256]{0:T(256)} %param.27) | copy-start | bytes 3076
  13.0 10.3 %copy-start.9 = (s32[256]{0:T(256)S(1)}, s32[256]{0:T(256)}, u32[]{:S(2)}) copy-start(s32[256]{0:T(256)} %param.26) | copy-start | bytes 3076
  13.0 104.9 %all-to-all-start = ((f32[16,256,256]{2,1,0:T(8,128)}), f32[16,256,256]{2,1,0:T(8,128)}, u32[]{:S(2)}, u32[]{:S(2)}) async-start(f32[16,256,256]{2,1,0:T(8,128)} %broadcast_in_dim.46), calls=%async_computation | async-start | bytes 8388608 | tf_op jit(solution)/shard_map/all_to_all | solution.py:29
  21.9 110.1 %all-gather.6.cloned.1.call-start = ((), (), s32[]{:S(2)}) async-start(), calls=%async_computation.2 | async-start | bytes 4718592 | tf_op jit(solution)/shard_map/all_gather | solution.py:23
  23.0 148.5 %all-gather.10.cloned.1.call-start = ((), (), s32[]{:S(2)}) async-start(), calls=%async_computation.4 | async-start | bytes 2396160 | tf_op jit(solution)/shard_map/all_gather | solution.py:51
  120.4 4.4 %copy-start.5 = (bf16[256,256]{1,0:T(8,128)(2,1)S(1)}, bf16[256,256]{1,0:T(8,128)(2,1)}, u32[]{:S(2)}) copy-start(bf16[256,256]{1,0:T(8,128)(2,1)} %param.25) | copy-start | bytes 393220
  120.4 4.4 %copy-start.6 = (bf16[256,256]{1,0:T(8,128)(2,1)S(1)}, bf16[256,256]{1,0:T(8,128)(2,1)}, u32[]{:S(2)}) copy-start(bf16[256,256]{1,0:T(8,128)(2,1)} %param.24) | copy-start | bytes 393220
  175.1 28.2 %copy-start.7 = (s32[4]{0:T(128)S(1)}, s32[4]{0:T(128)}, u32[]{:S(2)}) copy-start(s32[4]{0:T(128)} %param.20) | copy-start | bytes 52
  187.2 73.5 %all-to-all-start.1 = ((bf16[32,8,512]{2,1,0:T(8,128)(2,1)}), bf16[32,8,512]{2,1,0:T(8,128)(2,1)}, u32[]{:S(2)}, u32[]{:S(2)}) async-start(bf16[32,8,512]{2,1,0:T(8,128)(2,1)} %fusion.41), calls=%async_computation.1 | async-start | bytes 524288 | tf_op jit(solution)/shard_map/all_to_all | solution.py:77
Sparse Core Ops, SparseCore 0:
  10.1 63.4 all-gather.7
  75.7 56.2 all-gather.5
  134.1 37.3 all-gather.9
where the time goes:
time: 270 us; the launch traced here: 269 us
  waiting for transfers between devices  137 us (51%)
  matrix products  46.8 us (17%)
  other arithmetic  26.6 us (10%)
  starting transfers between devices  25 us (9%)
  between operations  14.2 us (5%)
  local copies, waits for them, and re-layouts  13.2 us (5%)
  blocking collectives  5.93 us (2%)
    all_to_all x1, waiting for transfers between devices, sent_to_all(): lax.all_to_all(jnp.broadcast_to(shard[None], (devices, *shard.shape)), ax...  94.3 us
    all_gather x1, waiting for transfers between devices, collected_together(): both, at, found = (lax.all_gather(jnp.concatenate(lines), axis), 0, {})  35.2 us
    dot_general x17, matrix products, online_update(): jnp.dot(weights.astype(jnp.bfloat16), values, preferred_element_type=jnp....  22.5 us
    dot_general x17, matrix products, online_update(): jnp.einsum('qd,kd->qk', queries, keys, preferred_element_type=jnp.float32)  22 us
    all_to_all x1, starting transfers between devices, sum_at_owner(): lax.all_to_all(cut_along(shard, dim, devices), axis, 0, 0, tiled=True)  16.1 us
    all_to_all x1, starting transfers between devices, sent_to_all(): lax.all_to_all(jnp.broadcast_to(shard[None], (devices, *shard.shape)), ax...  8.86 us
    all_gather x1, waiting for transfers between devices, side_by_side(): out = lax.all_gather(both, axis, axis=dim, tiled=True)  7.14 us
    all_gather x1, blocking collectives, collected_together(): both, at, found = (lax.all_gather(jnp.concatenate(lines), axis), 0, {})  5.93 us
  transfers between devices with their start and end apart: 5, of which 3 were waited for; matrix products, arithmetic and copies ran while one was open for 27% of the time, Pallas kernels for 0%

commit v1 on v0

v1 whole, which is shorter than its diff:
```python
import math

import jax
import jax.numpy as jnp
from jax import lax
from jax.experimental import pallas as pl
from jax.experimental.pallas import tpu as pltpu
from jax.sharding import Mesh
from jax.sharding import PartitionSpec as P

HQ = 64
KVH = 8
HD = 128
QBLK = 128
CTX = ("ctx_0", "ctx_1")
HEAD_CTX = ("head", "ctx_0", "ctx_1")
GROUP = HQ // KVH
SCALE = 1.0 / math.sqrt(HD)
SCALE2 = math.log2(math.e) / math.sqrt(HD)
MASKED = -1e30
FLOOR = -1e20

SMEM = pl.BlockSpec(memory_space=pltpu.SMEM)
VMEM = pl.BlockSpec(memory_space=pltpu.VMEM)


def cost(flops, moved, transcendentals=0):
    return pl.CostEstimate(flops=flops, bytes_accessed=moved, transcendentals=transcendentals)


def contract(a, b, dim_a, dim_b):
    return lax.dot_general(
        a, b, (((dim_a,), (dim_b,)), ((), ())), preferred_element_type=jnp.float32
    )


def pack_kernel(at_ref, kp, vp, kn, vn, kps, vps, kns, vns, rows_ref, span_ref):
    block = kp.shape[0]
    for n, ref in enumerate((kp, vp, kn, vn)):
        rows_ref[n * block : (n + 1) * block] = ref[...]

    @pl.when(at_ref[2] == 0)
    def _():
        span_ref[:block] = kps[...]
        span_ref[block:] = vps[...]

    @pl.when(at_ref[2] != 0)
    def _():
        span_ref[:block] = kns[...]
        span_ref[block:] = vns[...]


def pack(at, k_prefix, v_prefix, k_new, v_new):
    block = k_prefix.shape[0]
    arrays = (k_prefix, v_prefix, k_new, v_new)
    first = pl.BlockSpec((block, HD), lambda i, at: (0, at[0]))
    second = pl.BlockSpec((block, HD), lambda i, at: (0, at[1]))
    whole = lambda n: pl.BlockSpec((n * block, HD), lambda i, at: (0, 0))
    return pl.pallas_call(
        pack_kernel,
        grid_spec=pltpu.PrefetchScalarGridSpec(
            num_scalar_prefetch=1,
            grid=(1,),
            in_specs=[first] * 4 + [second] * 4,
            out_specs=[whole(4), whole(2)],
        ),
        out_shape=[
            jax.ShapeDtypeStruct((4 * block, HD), k_prefix.dtype),
            jax.ShapeDtypeStruct((2 * block, HD), k_prefix.dtype),
        ],
        cost_estimate=cost(1 << 20, 14 * block * HD * 2),
        name="pack",
    )(at, *arrays, *arrays)


def prefill_kernel(off_ref, seq_ref, q_ref, kv_ref, o_ref, m_ref, l_ref, acc_ref):
    src = pl.program_id(0)
    seq = seq_ref[0]
    rows = q_ref.shape[0]
    block = kv_ref.shape[1] // 4

    @pl.when(src == 0)
    def _():
        m_ref[...] = jnp.full_like(m_ref, FLOOR)
        l_ref[...] = jnp.zeros_like(l_ref)
        acc_ref[...] = jnp.zeros_like(acc_ref)

    def run(base, visible):
        keys = kv_ref[0, base : base + block]
        values = kv_ref[0, base + block : base + 2 * block]
        s = contract(keys, q_ref[...], 1, 1)
        if visible is not None:
            s = jnp.where(visible(), s, MASKED)
        m = m_ref[...]
        top = jnp.maximum(m, jnp.max(s, axis=0, keepdims=True))
        factor = jnp.exp2((m - top) * SCALE2)
        p = jnp.exp2((s - top) * SCALE2)
        m_ref[...] = top
        l_ref[...] = l_ref[...] * factor + jnp.sum(p, axis=0, keepdims=True)
        acc_ref[...] = acc_ref[...] * factor + contract(values, p.astype(jnp.bfloat16), 0, 0)

    def in_prefix():
        pos = src * block + lax.broadcasted_iota(jnp.int32, (block, rows), 0)
        part = lax.broadcasted_iota(jnp.int32, (1, rows), 1) // QBLK
        first = jnp.full((1, rows), off_ref[0], jnp.int32)
        for n in range(1, off_ref.shape[0]):
            first = jnp.where(part == n, off_ref[n], first)
        return pos >= first

    def causal():
        at = lax.broadcasted_iota(jnp.int32, (block, rows), 0)
        return at <= lax.broadcasted_iota(jnp.int32, (block, rows), 1)

    last = off_ref[0]
    for n in range(1, off_ref.shape[0]):
        last = jnp.maximum(last, off_ref[n])
    pl.when(src * block >= last)(lambda: run(0, None))
    pl.when(src * block < last)(lambda: run(0, in_prefix))
    pl.when(src < seq)(lambda: run(2 * block, None))
    pl.when(src == seq)(lambda: run(2 * block, causal))

    @pl.when(src == pl.num_programs(0) - 1)
    def _():
        o_ref[...] = jnp.transpose(acc_ref[...] / l_ref[...]).astype(o_ref.dtype)


def prefill(offsets, seq, q, cache):
    n, size, _ = cache.shape
    rows = q.shape[0]
    return pl.pallas_call(
        prefill_kernel,
        grid=(n,),
        out_shape=jax.ShapeDtypeStruct(q.shape, jnp.bfloat16),
        in_specs=[
            SMEM,
            SMEM,
            pl.BlockSpec((rows, HD), lambda i: (0, 0)),
            pl.BlockSpec((1, size, HD), lambda i: (i, 0, 0)),
        ],
        out_specs=pl.BlockSpec((rows, HD), lambda i: (0, 0)),
        scratch_shapes=[
            pltpu.VMEM((1, rows), jnp.float32),
            pltpu.VMEM((1, rows), jnp.float32),
            pltpu.VMEM((HD, rows), jnp.float32),
        ],
        compiler_params=pltpu.CompilerParams(dimension_semantics=("arbitrary",)),
        cost_estimate=cost(2 * rows * n * size * HD, n * size * HD * 2, rows * n * size // 2),
        name="prefill",
    )(offsets, seq, q, cache)


def sum_kernel(parts_ref, out_ref):
    total = jnp.sum(parts_ref[...], axis=0).astype(out_ref.dtype)
    for n in range(out_ref.shape[0]):
        out_ref[n] = total


def summed_for_all(parts):
    return pl.pallas_call(
        sum_kernel,
        out_shape=jax.ShapeDtypeStruct(parts.shape, jnp.bfloat16),
        in_specs=[VMEM],
        out_specs=VMEM,
        cost_estimate=cost(parts.size, parts.size * 6),
        name="sum_queries",
    )(parts)


def three_parts(x):
    high = x.astype(jnp.bfloat16)
    rest = x - high.astype(jnp.float32)
    middle = rest.astype(jnp.bfloat16)
    return (high, middle, (rest - middle.astype(jnp.float32)).astype(jnp.bfloat16))


def span_kernel(q_ref, span_ref, limit_ref, out_ref):
    rows = q_ref.shape[0]
    heads = q_ref.shape[1] // HD
    block = span_ref.shape[0] // 2
    keys, values = span_ref[:block], span_ref[block:]
    visible = lax.broadcasted_iota(jnp.int32, (rows, block), 1) < limit_ref[...]
    lane = lax.broadcasted_iota(jnp.int32, (rows, HD), 1)
    stats = jnp.zeros((rows, HD), jnp.float32)
    for h in range(heads):
        s = contract(q_ref[:, h * HD : (h + 1) * HD], keys, 1, 1)
        s = jnp.where(visible, s, MASKED)
        top = jnp.maximum(jnp.max(s, axis=1, keepdims=True), FLOOR)
        p = jnp.exp2((s - top) * SCALE2)
        total = jnp.sum(p, axis=1, keepdims=True)
        accum = contract(p.astype(jnp.bfloat16), values, 1, 0)
        out_ref[:, h * HD : (h + 1) * HD] = (
            accum / jnp.where(total > 0.0, total, 1.0)
        ).astype(out_ref.dtype)
        for n, part in enumerate(three_parts(top) + three_parts(total)):
            stats = jnp.where(lane == 6 * h + n, part.astype(jnp.float32), stats)
    out_ref[:, heads * HD :] = stats.astype(out_ref.dtype)


def span_attention(queries, span, limit):
    rows, width = queries.shape
    block = span.shape[0] // 2
    return pl.pallas_call(
        span_kernel,
        out_shape=jax.ShapeDtypeStruct((rows, width + HD), jnp.bfloat16),
        in_specs=[VMEM] * 3,
        out_specs=VMEM,
        cost_estimate=cost(4 * rows * width * block, (rows * width + block * HD) * 4),
        name="span_attention",
    )(queries, span, limit)


def merge_kernel(parts_ref, q_ref, k_ref, v_ref, out_ref):
    copies, rows, width = out_ref.shape
    heads = width // HD
    own_k = k_ref[...].astype(jnp.float32)
    own_v = v_ref[...].astype(jnp.float32)
    stats = parts_ref[:, :, width:].astype(jnp.float32)
    merged = []
    for h in range(heads):
        part = [stats[:, :, 6 * h + n : 6 * h + n + 1] for n in range(6)]
        tops = part[0] + part[1] + part[2]
        totals = part[3] + part[4] + part[5]
        q = q_ref[:, h * HD : (h + 1) * HD].astype(jnp.float32)
        own = jnp.sum(q * own_k, axis=1, keepdims=True)
        top = jnp.maximum(jnp.max(tops, axis=0), own)
        weights = jnp.exp2((tops - top[None]) * SCALE2) * totals
        own_w = jnp.exp2((own - top) * SCALE2)
        total = jnp.sum(weights, axis=0) + own_w
        values = parts_ref[:, :, h * HD : (h + 1) * HD].astype(jnp.float32)
        accum = jnp.sum(weights * values, axis=0)
        accum = accum + own_w.astype(jnp.bfloat16).astype(jnp.float32) * own_v
        merged.append((accum / total).astype(out_ref.dtype))
    whole = jnp.concatenate(merged, axis=1)
    for n in range(copies):
        out_ref[n] = whole


def merged_for_all(parts, queries, own_k, own_v):
    copies, rows, _ = parts.shape
    return pl.pallas_call(
        merge_kernel,
        out_shape=jax.ShapeDtypeStruct((copies, *queries.shape), jnp.bfloat16),
        in_specs=[VMEM] * 4,
        out_specs=VMEM,
        cost_estimate=cost(parts.size * 4, parts.size * 4),
        name="merge",
    )(parts, queries, own_k, own_v)


def body(
    q_new,
    k_prefix,
    v_prefix,
    k_new,
    v_new,
    block_offsets,
    dec_hidden,
    w_query,
    w_out,
    k_own,
    v_own,
    valid_len,
    parent,
):
    n_seq = lax.axis_size("seq")
    n_ctx = lax.axis_size(CTX)
    seq = lax.axis_index("seq")
    ctx = lax.axis_index(CTX)
    block = q_new.shape[0]
    rows = dec_hidden.shape[0]
    heads_dec = w_query.shape[2] // HD
    width = heads_dec * HD
    chunk = rows // n_ctx

    for_seq = ctx % n_seq
    at = jnp.stack([ctx // GROUP, for_seq * heads_dec // GROUP, ctx // n_seq]).astype(jnp.int32)
    mine, span = pack(at, k_prefix, v_prefix, k_new, v_new)
    partial_q = jnp.dot(
        dec_hidden, w_query.reshape(w_query.shape[0], -1), preferred_element_type=jnp.float32
    )
    parts = lax.all_to_all(partial_q.reshape(n_ctx, chunk, width), CTX, 0, 0, tiled=True)
    cache = lax.all_gather(mine, "seq")
    span = lax.ppermute(
        span,
        ("seq", *CTX),
        [
            ((c % n_seq) * n_ctx + s + n_seq * (c // n_seq), s * n_ctx + c)
            for s in range(n_seq)
            for c in range(n_ctx)
        ]
        if n_ctx == 2 * n_seq
        else None,
    )
    my_q = summed_for_all(parts)
    dec_q = lax.all_to_all(my_q, CTX, 0, 0, tiled=True).reshape(rows, width)
    limit = jnp.where(
        ctx < n_seq, valid_len - ctx * block, parent + 1 - (ctx - n_seq) * block
    ).reshape(rows, 1)
    local = span_attention(dec_q, span, limit)
    parts = lax.all_to_all(local.reshape(n_ctx, chunk, width + HD), CTX, 0, 0, tiled=True)
    kv_dec = seq * heads_dec // GROUP
    own_k = lax.dynamic_slice(k_own, (ctx * chunk, kv_dec * HD), (chunk, HD))
    own_v = lax.dynamic_slice(v_own, (ctx * chunk, kv_dec * HD), (chunk, HD))
    attn = merged_for_all(parts, my_q[0], own_k, own_v)
    attn = lax.all_to_all(attn, CTX, 0, 0, tiled=True).reshape(rows, width)
    summed = jnp.dot(
        attn, w_out.reshape(-1, w_out.shape[2]), preferred_element_type=jnp.float32
    ).astype(jnp.bfloat16)
    devices = lax.axis_size(("seq", "head"))
    tiles = lax.all_to_all(
        summed.reshape(devices, rows // devices, -1), ("seq", "head"), 0, 0, tiled=True
    )
    decoded = jnp.sum(tiles.astype(jnp.float32), axis=0).astype(jnp.bfloat16)
    prefill_out = prefill(block_offsets, seq.reshape(1).astype(jnp.int32), q_new, cache)
    return (prefill_out, decoded)


def solution(mesh):
    split = Mesh(
        mesh.devices.reshape(mesh.shape["seq"], mesh.shape["head"], 8, 2),
        ("seq", "head", "ctx_0", "ctx_1"),
    )
    return jax.shard_map(
        body,
        mesh=split,
        in_specs=(
            P("seq", HEAD_CTX),
            P("seq", "head"),
            P("seq", "head"),
            P("seq", "head"),
            P("seq", "head"),
            P("seq"),
            P(None, CTX),
            P(CTX, "head", "seq"),
            P("head", "seq", CTX),
            P(None, "head"),
            P(None, "head"),
            P(),
            P(),
        ),
        out_specs=(P("seq", HEAD_CTX), P(("seq", "head"), CTX)),
        check_vma=False,
    )
```

time: 270 us -> 137 us (0.51)
  waiting for transfers between devices: 137 us -> 27.2 us
  matrix products: 46.8 us -> 2.12 us
  blocking collectives: 5.93 us -> 40.4 us
  other arithmetic: 26.6 us -> 1.27 us
  Pallas kernels: 0 us -> 18.5 us
  local copies, waits for them, and re-layouts: 13.2 us -> 6.74 us
    all_to_all x2 -> x3, waiting for transfers between devices: 94.3 us -> 27.2 us  [the longest x1 13.8 us: body(): dec_q = lax.all_to_all(my_q, CTX, 0, 0, tiled=True).reshape(rows, width)]
    dot_general x35 -> x1, matrix products: 45.5 us -> 0.22 us  [body(): jnp.dot(attn, w_out.reshape(-1, w_out.shape[2]), preferred_element_type=j...]
    all_gather x3 -> x1, waiting for transfers between devices: 42.3 us -> 0.01 us  [body(): cache = lax.all_gather(mine, 'seq')]
    all_to_all x0 -> x2, blocking collectives: none -> 40.4 us  [the longest x1 28.3 us: body(): lax.all_to_all(summed.reshape(devices, rows // devices, -1), ('seq', 'hea...]
    pallas_call x0 -> x5, Pallas kernels: none -> 18.5 us  [the longest x1 9.39 us: prefill(): pl.pallas_call(prefill_kernel, grid=(n,), out_shape=jax.ShapeDtypeStruct(...]
    add x20 -> x0, other arithmetic: 8.08 us -> none  [the longest x8 4.61 us: body(): seq_idx * block + jnp.arange(block * per_dev, dtype=jnp.int32) // per_dev]
    reduce_sum x12 -> x1, other arithmetic: 8.3 us -> 0.65 us  [body(): decoded = jnp.sum(tiles.astype(jnp.float32), axis=0).astype(jnp.bfloat16)]
    all_gather x1 -> x0, blocking collectives: 5.93 us -> none  [collected_together(): both, at, found = (lax.all_gather(jnp.concatenate(lines), axis), 0, {})]
  transfers between devices with their start and end apart: 5 -> 5, of which waited for: 3 -> 3; matrix products, arithmetic and copies ran while one was open for 27% -> 5% of each run, Pallas kernels for 0% -> 5%
where the time goes in v1:
time: 137 us; the launch traced here: 136 us
  blocking collectives  40.4 us (29%)
  waiting for transfers between devices  27.2 us (20%)
  starting transfers between devices  25.5 us (19%)
  Pallas kernels  18.5 us (14%)
  between operations  14.2 us (10%)
  local copies, waits for them, and re-layouts  6.74 us (5%)
  matrix products  2.12 us (2%)
    all_to_all x1, blocking collectives, body(): lax.all_to_all(summed.reshape(devices, rows // devices, -1), ('seq', 'hea...  28.3 us
    all_to_all x1, waiting for transfers between devices, body(): dec_q = lax.all_to_all(my_q, CTX, 0, 0, tiled=True).reshape(rows, width)  13.8 us
    all_to_all x1, blocking collectives, body(): attn = lax.all_to_all(attn, CTX, 0, 0, tiled=True).reshape(rows, width)  12.1 us
    pallas_call x1, Pallas kernels, prefill(): pl.pallas_call(prefill_kernel, grid=(n,), out_shape=jax.ShapeDtypeStruct(...  9.39 us
    all_to_all x1, starting transfers between devices, body(): lax.all_to_all(partial_q.reshape(n_ctx, chunk, width), CTX, 0, 0, tiled=T...  8.66 us
    all_to_all x1, starting transfers between devices, body(): dec_q = lax.all_to_all(my_q, CTX, 0, 0, tiled=True).reshape(rows, width)  8.37 us
    all_to_all x1, waiting for transfers between devices, body(): lax.all_to_all(partial_q.reshape(n_ctx, chunk, width), CTX, 0, 0, tiled=T...  8.25 us
    all_to_all x1, starting transfers between devices, body(): lax.all_to_all(local.reshape(n_ctx, chunk, width + HD), CTX, 0, 0, tiled=...  6.78 us
  transfers between devices with their start and end apart: 5, of which 3 were waited for; matrix products, arithmetic and copies ran while one was open for 5% of the time, Pallas kernels for 5%

profile of v1, /device:TPU:1, one launch (start us, length us, event | category | flops | bytes accessed | tf_op | source)
XLA Modules:
  0.0 135.9 jit_solution(12503409219786399837)
XLA Ops:
  7.2 0.0 copy-start
  7.2 0.0 copy-start.7
  7.2 0.0 copy-start.6
  7.2 0.0 copy-start.4
  7.2 0.0 all-gather.3.cloned.1.call-start
  7.3 0.6 pad_add_fusion.at_ref
  7.9 2.9 %pack.1 = (bf16[2048,128]{1,0:T(8,128)(2,1)}, bf16[1024,128]{1,0:T(8,128)(2,1)}) custom-call(s32[3]{0:T(128)} %pad_add_fusion.at_ref, bf16[512,256]{1,0:T(8,128)(2,1)} %kps.1, bf16[512,256]{1,0:T(8,128)(2,1)} %vps.1, bf16[512,256]{1,0:T(8,128)(2,1)} %kns.1, bf16[512,256]{1,0:T(8,128)(2,1)} %vns.1, bf16[512,256]{1,0:T(8,128)(2,1)} %kps.1, ...), custom_call_target="tpu_custom_call" | custom-call | flops 1048576 | bytes 1835008 | tf_op jit(solution)/shard_map/pack/pallas_call | solution.py:59
  10.8 0.0 all-gather.3.cloned.1.call-update
  10.8 0.0 copy-done
  10.8 1.9 %fusion.2 = f32[16,16,256]{2,1,0:T(8,128)} fusion(bf16[16,16,512]{2,1,0:T(8,128)(2,1)S(1)} %bitcast.22, bf16[512,1,256]{2,0,1:T(8,128)(2,1)} %param.20), kind=kOutput, calls=%fused_computation.3 | convolution fusion | flops 67108864 | bytes 786432 | tf_op jit(solution)/shard_map/dot_general | solution.py:278
  12.7 8.7 %all-to-all-start = ((f32[16,16,256]{2,1,0:T(8,128)}), f32[16,16,256]{2,1,0:T(8,128)S(1)}, u32[]{:S(2)}, u32[]{:S(2)}) async-start(f32[16,16,256]{2,1,0:T(8,128)} %fusion.2), calls=%async_computation | async-start | bytes 524288 | tf_op jit(solution)/shard_map/all_to_all | solution.py:281
  21.4 1.6 %collective-permute-start = (bf16[1024,128]{1,0:T(8,128)(2,1)}, bf16[1024,128]{1,0:T(8,128)(2,1)S(1)}, u32[]{:S(2)}, u32[]{:S(2)}) collective-permute-start(bf16[1024,128]{1,0:T(8,128)(2,1)} %get-tuple-element.5), channel_id=1, source_target_pairs={{0,0},{64,1},{128,2},{192,3},{256,4},{320,5},{384,6},{448,7},{8,8}... | collective-permute-start | bytes 786440 | tf_op jit(solution)/shard_map/ppermute | solution.py:283
  23.0 8.2 %all-to-all-done.parts_ref = f32[16,16,256]{2,1,0:T(8,128)S(1)} async-done(((f32[16,16,256]{2,1,0:T(8,128)}), f32[16,16,256]{2,1,0:T(8,128)S(1)}, u32[]{:S(2)}, u32[]{:S(2)}) %all-to-all-start) | async-done | bytes 262176 | tf_op jit(solution)/shard_map/all_to_all | solution.py:281
  31.3 0.0 copy-start.1
  31.3 0.7 copy-done.1
  32.0 1.6 %sum_queries.1 = bf16[16,16,256]{2,1,0:T(8,128)(2,1)} custom-call(f32[16,16,256]{2,1,0:T(8,128)} %copy-done.1), custom_call_target="tpu_custom_call" | custom-call | flops 65536 | bytes 393216 | tf_op jit(solution)/shard_map/sum_queries/pallas_call | solution.py:159
  33.6 8.4 %all-to-all-start.1 = ((bf16[16,16,256]{2,1,0:T(8,128)(2,1)}), bf16[16,16,256]{2,1,0:T(8,128)(2,1)S(1)}, u32[]{:S(2)}, u32[]{:S(2)}) async-start(bf16[16,16,256]{2,1,0:T(8,128)(2,1)} %sum_queries.1), calls=%async_computation.1 | async-start | bytes 262144 | tf_op jit(solution)/shard_map/all_to_all | solution.py:295
  42.0 0.0 copy-done.7
  42.0 0.0 copy-done.6
  42.0 0.8 copy.15.limit_ref
  42.8 0.0 collective-permute-done.span_ref
  42.8 0.0 copy-start.5
  42.8 13.8 %all-to-all-done.1 = bf16[16,16,256]{2,1,0:T(8,128)(2,1)S(1)} async-done(((bf16[16,16,256]{2,1,0:T(8,128)(2,1)}), bf16[16,16,256]{2,1,0:T(8,128)(2,1)S(1)}, u32[]{:S(2)}, u32[]{:S(2)}) %all-to-all-start.1) | async-done | bytes 131104 | tf_op jit(solution)/shard_map/all_to_all | solution.py:295
  56.6 0.0 copy-start.3
  56.6 0.0 copy-done.5
  56.6 0.7 copy-done.3
  57.3 2.6 %span_attention.1 = bf16[256,384]{1,0:T(8,128)(2,1)} custom-call(bf16[256,256]{1,0:T(8,128)(2,1)} %bitcast.25, bf16[1024,128]{1,0:T(8,128)(2,1)} %copy-done.5, s32[256,1]{1,0:T(8,128)} %copy.15.limit_ref), custom_call_target="tpu_custom_call" | custom-call | flops 134217728 | bytes 524288 | tf_op jit(solution)/shard_map/span_attention/pallas_call | solution.py:202
  59.9 6.8 %all-to-all-start.2 = ((bf16[16,16,384]{2,1,0:T(8,128)(2,1)}), bf16[16,16,384]{2,1,0:T(8,128)(2,1)S(1)}, u32[]{:S(2)}, u32[]{:S(2)}) async-start(bf16[16,16,384]{2,1,0:T(8,128)(2,1)} %bitcast.23), calls=%async_computation.2 | async-start | bytes 393216 | tf_op jit(solution)/shard_map/all_to_all | solution.py:300
  66.7 1.3 dynamic_slice.6.k_ref
  68.0 1.3 dynamic_slice.7.v_ref
  69.3 1.3 slice_bitcast_fusion.q_ref
  70.6 5.2 %all-to-all-done.2.parts_ref = bf16[16,16,384]{2,1,0:T(8,128)(2,1)S(1)} async-done(((bf16[16,16,384]{2,1,0:T(8,128)(2,1)}), bf16[16,16,384]{2,1,0:T(8,128)(2,1)S(1)}, u32[]{:S(2)}, u32[]{:S(2)}) %all-to-all-start.2) | async-done | bytes 196640 | tf_op jit(solution)/shard_map/all_to_all | solution.py:300
  75.7 0.0 copy-start.2
  75.7 0.7 copy-done.2
  76.4 1.9 %merge.1 = bf16[16,16,256]{2,1,0:T(8,128)(2,1)} custom-call(bf16[16,16,384]{2,1,0:T(8,128)(2,1)} %copy-done.2, bf16[16,256]{1,0:T(8,128)(2,1)} %slice_bitcast_fusion.q_ref, bf16[16,128]{1,0:T(8,128)(2,1)} %dynamic_slice.6.k_ref, bf16[16,128]{1,0:T(8,128)(2,1)} %dynamic_slice.7.v_ref), custom_call_target="tpu_custom_call" | custom-call | flops 393216 | bytes 393216 | tf_op jit(solution)/shard_map/merge/pallas_call | solution.py:240
  78.4 12.1 %all_to_all.25 = bf16[16,16,256]{2,1,0:T(8,128)(2,1)S(1)} all-to-all(bf16[16,16,256]{2,1,0:T(8,128)(2,1)} %merge.1), channel_id=1, replica_groups=mesh['seq'=8,'head'=4,'ctx_0'=8,'ctx_1'=2] {'ctx_0','ctx_1'}, dimensions={0} | all-to-all | bytes 262144 | tf_op jit(solution)/shard_map/all_to_all | solution.py:305
  90.4 0.0 copy-done.4
  90.4 0.2 fusion
  90.7 28.3 %all_to_all.26 = bf16[32,8,512]{2,1,0:T(8,128)(2,1)S(1)} all-to-all(bf16[32,8,512]{2,1,0:T(8,128)(2,1)S(1)} %fusion), channel_id=1, replica_groups=mesh['seq'=8,'head'=4,'ctx_0'=8,'ctx_1'=2] {'seq','head'}, dimensions={0} | all-to-all | bytes 524288 | tf_op jit(solution)/shard_map/all_to_all | solution.py:310
  119.0 0.6 reduce_sum.12
  119.6 0.0 all-gather.3.cloned.1.call-done
  119.6 9.4 %prefill.1 = bf16[512,128]{1,0:T(8,128)(2,1)} custom-call(s32[4]{0:T(128)} %off_ref.1, s32[1]{0:T(128)} %bitcast.seq_ref, bf16[512,128]{1,0:T(8,128)(2,1)} %q_ref.1, bf16[8,2048,128]{2,1,0:T(8,128)(2,1)} %bitcast.27), custom_call_target="tpu_custom_call" | custom-call | flops 2147483648 | bytes 4194304 | tf_op jit(solution)/shard_map/prefill/pallas_call | solution.py:130
  (1 shorter events, 0.0 us)
Async XLA Ops:
  7.2 3.7 %copy-start = (bf16[256,512]{1,0:T(8,128)(2,1)S(1)}, bf16[256,512]{1,0:T(8,128)(2,1)}, u32[]{:S(2)}) copy-start(bf16[256,512]{1,0:T(8,128)(2,1)} %param.19) | copy-start | bytes 786436
  7.2 34.8 %copy-start.7 = (s32[256]{0:T(256)S(1)}, s32[256]{0:T(256)}, u32[]{:S(2)}) copy-start(s32[256]{0:T(256)} %param.24) | copy-start | bytes 3076
  7.2 34.8 %copy-start.6 = (s32[256]{0:T(256)S(1)}, s32[256]{0:T(256)}, u32[]{:S(2)}) copy-start(s32[256]{0:T(256)} %param.25) | copy-start | bytes 3076
  7.2 83.2 %copy-start.4 = (bf16[1,256,512]{2,1,0:T(8,128)(2,1)S(1)}, bf16[1,256,512]{2,1,0:T(8,128)(2,1)}, u32[]{:S(2)}) copy-start(bf16[1,256,512]{2,1,0:T(8,128)(2,1)} %param.21) | copy-start | bytes 786436
  7.2 112.4 %all-gather.3.cloned.1.call-start = ((), (), s32[]{:S(2)}) async-start(), calls=%async_computation.5 | async-start | bytes 4718592 | tf_op jit(solution)/shard_map/all_gather | solution.py:282
  12.7 18.5 %all-to-all-start = ((f32[16,16,256]{2,1,0:T(8,128)}), f32[16,16,256]{2,1,0:T(8,128)S(1)}, u32[]{:S(2)}, u32[]{:S(2)}) async-start(f32[16,16,256]{2,1,0:T(8,128)} %fusion.2), calls=%async_computation | async-start | bytes 524288 | tf_op jit(solution)/shard_map/all_to_all | solution.py:281
  21.4 21.4 %collective-permute-start = (bf16[1024,128]{1,0:T(8,128)(2,1)}, bf16[1024,128]{1,0:T(8,128)(2,1)S(1)}, u32[]{:S(2)}, u32[]{:S(2)}) collective-permute-start(bf16[1024,128]{1,0:T(8,128)(2,1)} %get-tuple-element.5), channel_id=1, source_target_pairs={{0,0},{64,1},{128,2},{192,3},{256,4},{320,5},{384,6},{448,7},{8,8}... | collective-permute-start | bytes 786440 | tf_op jit(solution)/shard_map/ppermute | solution.py:283
  31.3 0.7 copy-start.1
  33.6 23.0 %all-to-all-start.1 = ((bf16[16,16,256]{2,1,0:T(8,128)(2,1)}), bf16[16,16,256]{2,1,0:T(8,128)(2,1)S(1)}, u32[]{:S(2)}, u32[]{:S(2)}) async-start(bf16[16,16,256]{2,1,0:T(8,128)(2,1)} %sum_queries.1), calls=%async_computation.1 | async-start | bytes 262144 | tf_op jit(solution)/shard_map/all_to_all | solution.py:295
  42.8 13.8 %copy-start.5 = (bf16[1024,128]{1,0:T(8,128)(2,1)}, bf16[1024,128]{1,0:T(8,128)(2,1)S(1)}, u32[]{:S(2)}) copy-start(bf16[1024,128]{1,0:T(8,128)(2,1)S(1)} %collective-permute-done.span_ref) | copy-start | bytes 786436
  56.6 0.7 copy-start.3
  59.9 15.8 %all-to-all-start.2 = ((bf16[16,16,384]{2,1,0:T(8,128)(2,1)}), bf16[16,16,384]{2,1,0:T(8,128)(2,1)S(1)}, u32[]{:S(2)}, u32[]{:S(2)}) async-start(bf16[16,16,384]{2,1,0:T(8,128)(2,1)} %bitcast.23), calls=%async_computation.2 | async-start | bytes 393216 | tf_op jit(solution)/shard_map/all_to_all | solution.py:300
  75.7 0.7 copy-start.2
Sparse Core Ops, SparseCore 0:
  11.0 77.2 all-gather.2

commit v2 on v1

--- a/solution.py
+++ b/solution.py
@@ -15,7 +15,6 @@
 CTX = ("ctx_0", "ctx_1")
 HEAD_CTX = ("head", "ctx_0", "ctx_1")
 GROUP = HQ // KVH
-SCALE = 1.0 / math.sqrt(HD)
 SCALE2 = math.log2(math.e) / math.sqrt(HD)
 MASKED = -1e30
 FLOOR = -1e20
@@ -34,43 +33,26 @@
     )
 
 
-def pack_kernel(at_ref, kp, vp, kn, vn, kps, vps, kns, vns, rows_ref, span_ref):
+def pack_kernel(at_ref, kp, vp, kn, vn, rows_ref):
     block = kp.shape[0]
     for n, ref in enumerate((kp, vp, kn, vn)):
         rows_ref[n * block : (n + 1) * block] = ref[...]
 
-    @pl.when(at_ref[2] == 0)
-    def _():
-        span_ref[:block] = kps[...]
-        span_ref[block:] = vps[...]
-
-    @pl.when(at_ref[2] != 0)
-    def _():
-        span_ref[:block] = kns[...]
-        span_ref[block:] = vns[...]
-
 
 def pack(at, k_prefix, v_prefix, k_new, v_new):
     block = k_prefix.shape[0]
-    arrays = (k_prefix, v_prefix, k_new, v_new)
-    first = pl.BlockSpec((block, HD), lambda i, at: (0, at[0]))
-    second = pl.BlockSpec((block, HD), lambda i, at: (0, at[1]))
-    whole = lambda n: pl.BlockSpec((n * block, HD), lambda i, at: (0, 0))
     return pl.pallas_call(
         pack_kernel,
         grid_spec=pltpu.PrefetchScalarGridSpec(
             num_scalar_prefetch=1,
             grid=(1,),
-            in_specs=[first] * 4 + [second] * 4,
-            out_specs=[whole(4), whole(2)],
+            in_specs=[pl.BlockSpec((block, HD), lambda i, at: (0, at[0]))] * 4,
+            out_specs=pl.BlockSpec((4 * block, HD), lambda i, at: (0, 0)),
         ),
-        out_shape=[
-            jax.ShapeDtypeStruct((4 * block, HD), k_prefix.dtype),
-            jax.ShapeDtypeStruct((2 * block, HD), k_prefix.dtype),
-        ],
-        cost_estimate=cost(1 << 20, 14 * block * HD * 2),
+        out_shape=jax.ShapeDtypeStruct((4 * block, HD), k_prefix.dtype),
+        cost_estimate=cost(1 << 20, 8 * block * HD * 2),
         name="pack",
-    )(at, *arrays, *arrays)
+    )(at, k_prefix, v_prefix, k_new, v_new)
 
 
 def prefill_kernel(off_ref, seq_ref, q_ref, kv_ref, o_ref, m_ref, l_ref, acc_ref):
@@ -155,10 +137,10 @@
         out_ref[n] = total
 
 
-def summed_for_all(parts):
+def summed_for_all(parts, copies):
     return pl.pallas_call(
         sum_kernel,
-        out_shape=jax.ShapeDtypeStruct(parts.shape, jnp.bfloat16),
+        out_shape=jax.ShapeDtypeStruct((copies, *parts.shape[1:]), jnp.bfloat16),
         in_specs=[VMEM],
         out_specs=VMEM,
         cost_estimate=cost(parts.size, parts.size * 6),
@@ -173,44 +155,70 @@
     return (high, middle, (rest - middle.astype(jnp.float32)).astype(jnp.bfloat16))
 
 
-def span_kernel(q_ref, span_ref, limit_ref, out_ref):
-    rows = q_ref.shape[0]
-    heads = q_ref.shape[1] // HD
-    block = span_ref.shape[0] // 2
-    keys, values = span_ref[:block], span_ref[block:]
-    visible = lax.broadcasted_iota(jnp.int32, (rows, block), 1) < limit_ref[...]
-    lane = lax.broadcasted_iota(jnp.int32, (rows, HD), 1)
-    stats = jnp.zeros((rows, HD), jnp.float32)
-    for h in range(heads):
-        s = contract(q_ref[:, h * HD : (h + 1) * HD], keys, 1, 1)
-        s = jnp.where(visible, s, MASKED)
-        top = jnp.maximum(jnp.max(s, axis=1, keepdims=True), FLOOR)
-        p = jnp.exp2((s - top) * SCALE2)
-        total = jnp.sum(p, axis=1, keepdims=True)
-        accum = contract(p.astype(jnp.bfloat16), values, 1, 0)
-        out_ref[:, h * HD : (h + 1) * HD] = (
-            accum / jnp.where(total > 0.0, total, 1.0)
-        ).astype(out_ref.dtype)
-        for n, part in enumerate(three_parts(top) + three_parts(total)):
-            stats = jnp.where(lane == 6 * h + n, part.astype(jnp.float32), stats)
-    out_ref[:, heads * HD :] = stats.astype(out_ref.dtype)
-
-
-def span_attention(queries, span, limit):
-    rows, width = queries.shape
-    block = span.shape[0] // 2
-    return pl.pallas_call(
-        span_kernel,
-        out_shape=jax.ShapeDtypeStruct((rows, width + HD), jnp.bfloat16),
-        in_specs=[VMEM] * 3,
+def rows_kernel(q_ref, kp_ref, vp_ref, kn_ref, vn_ref, limit_ref, out_ref):
+    owners, chunk, width = q_ref.shape
+    heads = width // HD
+    cached = kp_ref.shape[1] // HD
+    near = owners // cached
+    block = kp_ref.shape[0]
+    count = near * heads * chunk
+    lane = lax.broadcasted_iota(jnp.int32, (chunk, HD), 1)
+    at = lax.broadcasted_iota(jnp.int32, (count, block), 1)
+    limits = jnp.concatenate([limit_ref[...]] * (near * heads), axis=0)
+    for kv in range(cached):
+        cols = slice(kv * HD, (kv + 1) * HD)
+        q = jnp.concatenate(
+            [
+                q_ref[owner, :, h * HD : (h + 1) * HD]
+                for owner in range(kv * near, (kv + 1) * near)
+                for h in range(heads)
+            ],
+            axis=0,
+        )
+        s = [
+            jnp.where(at < limits[:, n : n + 1], contract(q, keys[:, cols], 1, 1), MASKED)
+            for n, keys in enumerate((kp_ref, kn_ref))
+        ]
+        top = jnp.maximum(
+            jnp.maximum(
+                jnp.max(s[0], axis=1, keepdims=True), jnp.max(s[1], axis=1, keepdims=True)
+            ),
+            FLOOR,
+        )
+        p = [jnp.exp2((x - top) * SCALE2) for x in s]
+        total = jnp.sum(p[0], axis=1, keepdims=True) + jnp.sum(p[1], axis=1, keepdims=True)
+        accum = contract(p[0].astype(jnp.bfloat16), vp_ref[:, cols], 1, 0) + contract(
+            p[1].astype(jnp.bfloat16), vn_ref[:, cols], 1, 0
+        )
+        values = accum / jnp.where(total > 0.0, total, 1.0)
+        parts = three_parts(top) + three_parts(total)
+        for n in range(near):
+            stats = jnp.zeros((chunk, HD), jnp.float32)
+            for h in range(heads):
+                here = slice((n * heads + h) * chunk, (n * heads + h + 1) * chunk)
+                out_ref[kv * near + n, :, h * HD : (h + 1) * HD] = values[here].astype(
+                    out_ref.dtype
+                )
+                for k, part in enumerate(parts):
+                    stats = jnp.where(lane == 6 * h + k, part[here].astype(jnp.float32), stats)
+            out_ref[kv * near + n, :, width:] = stats.astype(out_ref.dtype)
+
+
+def rows_attention(queries, k_prefix, v_prefix, k_new, v_new, limit):
+    owners, chunk, width = queries.shape
+    block = k_prefix.shape[0]
+    return pl.pallas_call(
+        rows_kernel,
+        out_shape=jax.ShapeDtypeStruct((owners, chunk, width + HD), jnp.bfloat16),
+        in_specs=[VMEM] * 6,
         out_specs=VMEM,
-        cost_estimate=cost(4 * rows * width * block, (rows * width + block * HD) * 4),
-        name="span_attention",
-    )(queries, span, limit)
-
-
-def merge_kernel(parts_ref, q_ref, k_ref, v_ref, out_ref):
-    copies, rows, width = out_ref.shape
+        cost_estimate=cost(8 * queries.size * block, k_prefix.size * 8),
+        name="rows_attention",
+    )(queries, k_prefix, v_prefix, k_new, v_new, limit)
+
+
+def merge_kernel(at_ref, parts_ref, q_ref, k_ref, v_ref, out_ref):
+    copies, _, width = out_ref.shape
     heads = width // HD
     own_k = k_ref[...].astype(jnp.float32)
     own_v = v_ref[...].astype(jnp.float32)
@@ -220,7 +228,7 @@
         part = [stats[:, :, 6 * h + n : 6 * h + n + 1] for n in range(6)]
         tops = part[0] + part[1] + part[2]
         totals = part[3] + part[4] + part[5]
-        q = q_ref[:, h * HD : (h + 1) * HD].astype(jnp.float32)
+        q = q_ref[0, :, h * HD : (h + 1) * HD].astype(jnp.float32)
         own = jnp.sum(q * own_k, axis=1, keepdims=True)
         top = jnp.maximum(jnp.max(tops, axis=0), own)
         weights = jnp.exp2((tops - top[None]) * SCALE2) * totals
@@ -235,16 +243,26 @@
         out_ref[n] = whole
 
 
-def merged_for_all(parts, queries, own_k, own_v):
-    copies, rows, _ = parts.shape
+def merged_for_all(at, parts, queries, k_own, v_own, copies):
+    sources, chunk, width = parts.shape
+    own = pl.BlockSpec((chunk, HD), lambda i, at: (at[1], at[2]))
     return pl.pallas_call(
         merge_kernel,
-        out_shape=jax.ShapeDtypeStruct((copies, *queries.shape), jnp.bfloat16),
-        in_specs=[VMEM] * 4,
-        out_specs=VMEM,
+        grid_spec=pltpu.PrefetchScalarGridSpec(
+            num_scalar_prefetch=1,
+            grid=(1,),
+            in_specs=[
+                pl.BlockSpec((sources, chunk, width), lambda i, at: (0, 0, 0)),
+                pl.BlockSpec((1, chunk, width - HD), lambda i, at: (0, 0, 0)),
+                own,
+                own,
+            ],
+            out_specs=pl.BlockSpec((copies, chunk, width - HD), lambda i, at: (0, 0, 0)),
+        ),
+        out_shape=jax.ShapeDtypeStruct((copies, chunk, width - HD), jnp.bfloat16),
         cost_estimate=cost(parts.size * 4, parts.size * 4),
         name="merge",
-    )(parts, queries, own_k, own_v)
+    )(at, parts, queries, k_own, v_own)
 
 
 def body(
@@ -272,36 +290,21 @@
     width = heads_dec * HD
     chunk = rows // n_ctx
 
-    for_seq = ctx % n_seq
-    at = jnp.stack([ctx // GROUP, for_seq * heads_dec // GROUP, ctx // n_seq]).astype(jnp.int32)
-    mine, span = pack(at, k_prefix, v_prefix, k_new, v_new)
+    at = jnp.stack([ctx // GROUP, ctx, seq * heads_dec // GROUP]).astype(jnp.int32)
+    mine = pack(at, k_prefix, v_prefix, k_new, v_new)
+    cache = lax.all_gather(mine, "seq")
+
     partial_q = jnp.dot(
         dec_hidden, w_query.reshape(w_query.shape[0], -1), preferred_element_type=jnp.float32
     )
     parts = lax.all_to_all(partial_q.reshape(n_ctx, chunk, width), CTX, 0, 0, tiled=True)
-    cache = lax.all_gather(mine, "seq")
-    span = lax.ppermute(
-        span,
-        ("seq", *CTX),
-        [
-            ((c % n_seq) * n_ctx + s + n_seq * (c // n_seq), s * n_ctx + c)
-            for s in range(n_seq)
-            for c in range(n_ctx)
-        ]
-        if n_ctx == 2 * n_seq
-        else None,
-    )
-    my_q = summed_for_all(parts)
-    dec_q = lax.all_to_all(my_q, CTX, 0, 0, tiled=True).reshape(rows, width)
-    limit = jnp.where(
-        ctx < n_seq, valid_len - ctx * block, parent + 1 - (ctx - n_seq) * block
-    ).reshape(rows, 1)
-    local = span_attention(dec_q, span, limit)
-    parts = lax.all_to_all(local.reshape(n_ctx, chunk, width + HD), CTX, 0, 0, tiled=True)
-    kv_dec = seq * heads_dec // GROUP
-    own_k = lax.dynamic_slice(k_own, (ctx * chunk, kv_dec * HD), (chunk, HD))
-    own_v = lax.dynamic_slice(v_own, (ctx * chunk, kv_dec * HD), (chunk, HD))
-    attn = merged_for_all(parts, my_q[0], own_k, own_v)
+    my_q = summed_for_all(parts, n_seq)
+    dec_q = lax.all_to_all(my_q, "seq", 0, 0, tiled=True)
+    limit = jnp.stack([valid_len, parent + 1], axis=1) - seq * block
+    limit = lax.dynamic_slice_in_dim(limit, ctx * chunk, chunk, 0)
+    local = rows_attention(dec_q, k_prefix, v_prefix, k_new, v_new, limit)
+    parts = lax.all_to_all(local, "seq", 0, 0, tiled=True)
+    attn = merged_for_all(at, parts, my_q, k_own, v_own, n_ctx)
     attn = lax.all_to_all(attn, CTX, 0, 0, tiled=True).reshape(rows, width)
     summed = jnp.dot(
         attn, w_out.reshape(-1, w_out.shape[2]), preferred_element_type=jnp.float32

time: 137 us -> 122 us (0.89)
  blocking collectives: 40.4 us -> 66.3 us
  waiting for transfers between devices: 27.2 us -> 6.07 us
  starting transfers between devices: 25.5 us -> 10.6 us
  local copies, waits for them, and re-layouts: 6.74 us -> 1.32 us
  other arithmetic: 1.27 us -> 2.68 us
    all_to_all x0 -> x2, blocking collectives: none -> 31.4 us  [the longest x1 18.7 us: body(): lax.all_to_all(partial_q.reshape(n_ctx, chunk, width), CTX, 0, 0, tiled=T...]
    all_to_all x3 -> x1, waiting for transfers between devices: 27.2 us -> 6.05 us  [body(): dec_q = lax.all_to_all(my_q, 'seq', 0, 0, tiled=True)]
    all_to_all x3 -> x1, starting transfers between devices: 23.8 us -> 10.5 us  [body(): dec_q = lax.all_to_all(my_q, 'seq', 0, 0, tiled=True)]
    all_to_all x1, blocking collectives: 28.3 us -> 22.9 us  [body(): lax.all_to_all(summed.reshape(devices, rows // devices, -1), ('seq', 'hea...]
    dynamic_slice x2 -> x0, local copies, waits for them, and re-layouts: 2.57 us -> none  [the longest x1 1.29 us: body(): own_k = lax.dynamic_slice(k_own, (ctx * chunk, kv_dec * HD), (chunk, HD))]
    ppermute x1 -> x0, starting transfers between devices: 1.61 us -> none  [body(): lax.ppermute(span, ('seq', *CTX), [(c % n_seq * n_ctx + s + n_seq * (c //...]
  transfers between devices with their start and end apart: 5 -> 2, of which waited for: 3 -> 1; matrix products, arithmetic and copies ran while one was open for 5% -> 3% of each run, Pallas kernels for 5% -> 6%
where the time goes in v2:
time: 122 us; the launch traced here: 121 us
  blocking collectives  66.3 us (54%)
  Pallas kernels  18.8 us (15%)
  between operations  14.1 us (12%)
  starting transfers between devices  10.6 us (9%)
  waiting for transfers between devices  6.07 us (5%)
  other arithmetic  2.68 us (2%)
  matrix products  1.39 us (1%)
  local copies, waits for them, and re-layouts  1.32 us (1%)
    all_to_all x1, blocking collectives, body(): lax.all_to_all(summed.reshape(devices, rows // devices, -1), ('seq', 'hea...  22.9 us
    all_to_all x1, blocking collectives, body(): lax.all_to_all(partial_q.reshape(n_ctx, chunk, width), CTX, 0, 0, tiled=T...  18.7 us
    all_to_all x1, blocking collectives, body(): parts = lax.all_to_all(local, 'seq', 0, 0, tiled=True)  12.7 us
    all_to_all x1, blocking collectives, body(): attn = lax.all_to_all(attn, CTX, 0, 0, tiled=True).reshape(rows, width)  12.1 us
    all_to_all x1, starting transfers between devices, body(): dec_q = lax.all_to_all(my_q, 'seq', 0, 0, tiled=True)  10.5 us
    pallas_call x1, Pallas kernels, prefill(): pl.pallas_call(prefill_kernel, grid=(n,), out_shape=jax.ShapeDtypeStruct(...  9.38 us
    all_to_all x1, waiting for transfers between devices, body(): dec_q = lax.all_to_all(my_q, 'seq', 0, 0, tiled=True)  6.05 us
    pallas_call x1, Pallas kernels, rows_attention(): pl.pallas_call(rows_kernel, out_shape=jax.ShapeDtypeStruct((owners, chunk...  2.74 us
  transfers between devices with their start and end apart: 2, of which 1 were waited for; matrix products, arithmetic and copies ran while one was open for 3% of the time, Pallas kernels for 6%

profile of v2, /device:TPU:1, one launch (start us, length us, event | category | flops | bytes accessed | tf_op | source)
XLA Modules:
  0.0 121.3 jit_solution(916698329200647585)
XLA Ops:
  7.2 0.0 copy-start
  7.2 0.0 copy-start.2
  7.2 0.0 all-gather.3.cloned.1.call-start
  7.3 0.6 pad_add_fusion.at_ref
  7.9 2.6 %pack.1 = bf16[2048,128]{1,0:T(8,128)(2,1)} custom-call(s32[3]{0:T(128)} %pad_add_fusion.at_ref, bf16[512,256]{1,0:T(8,128)(2,1)} %kp_ref.1, bf16[512,256]{1,0:T(8,128)(2,1)} %vp_ref.1, bf16[512,256]{1,0:T(8,128)(2,1)} %kn_ref.1, bf16[512,256]{1,0:T(8,128)(2,1)} %vn_ref.1), custom_call_target="tpu_custom_call" | custom-call | flops 1048576 | bytes 1048576 | tf_op jit(solution)/shard_map/pack/pallas_call | solution.py:44
  10.5 0.0 all-gather.3.cloned.1.call-update
  10.5 0.0 copy-done
  10.5 1.2 fusion.2
  11.7 18.7 %all_to_all.25.parts_ref = f32[16,16,256]{2,1,0:T(8,128)} all-to-all(f32[16,16,256]{2,1,0:T(8,128)S(1)} %fusion.2), channel_id=1, replica_groups=mesh['seq'=8,'head'=4,'ctx_0'=8,'ctx_1'=2] {'ctx_0','ctx_1'}, dimensions={0} | all-to-all | bytes 524288 | tf_op jit(solution)/shard_map/all_to_all | solution.py:300
  30.4 1.6 %sum_queries.1.q_ref = bf16[8,16,256]{2,1,0:T(8,128)(2,1)} custom-call(f32[16,16,256]{2,1,0:T(8,128)} %all_to_all.25.parts_ref), custom_call_target="tpu_custom_call" | custom-call | flops 65536 | bytes 393216 | tf_op jit(solution)/shard_map/sum_queries/pallas_call | solution.py:141
  31.9 10.5 %all-to-all-start.1 = ((bf16[8,16,256]{2,1,0:T(8,128)(2,1)}), bf16[8,16,256]{2,1,0:T(8,128)(2,1)S(1)}, u32[]{:S(2)}, u32[]{:S(2)}) async-start(bf16[8,16,256]{2,1,0:T(8,128)(2,1)} %sum_queries.1.q_ref), calls=%async_computation.1 | async-start | bytes 131072 | tf_op jit(solution)/shard_map/all_to_all | solution.py:302
  42.5 0.7 broadcast_add_fusion
  43.1 0.7 fusion.5
  43.9 0.7 copy.20.limit_ref
  44.6 6.1 %all-to-all-done.1.q_ref = bf16[8,16,256]{2,1,0:T(8,128)(2,1)S(1)} async-done(((bf16[8,16,256]{2,1,0:T(8,128)(2,1)}), bf16[8,16,256]{2,1,0:T(8,128)(2,1)S(1)}, u32[]{:S(2)}, u32[]{:S(2)}) %all-to-all-start.1) | async-done | bytes 65568 | tf_op jit(solution)/shard_map/all_to_all | solution.py:302
  50.6 0.0 copy-start.1
  50.6 0.6 copy-done.1
  51.2 2.7 %rows_attention.1 = bf16[8,16,384]{2,1,0:T(8,128)(2,1)} custom-call(bf16[8,16,256]{2,1,0:T(8,128)(2,1)} %copy-done.1, bf16[512,256]{1,0:T(8,128)(2,1)} %kp_ref.1, bf16[512,256]{1,0:T(8,128)(2,1)} %vp_ref.1, bf16[512,256]{1,0:T(8,128)(2,1)} %kn_ref.1, bf16[512,256]{1,0:T(8,128)(2,1)} %vn_ref.1, s32[16,2]{1,0:T(8,128)} %copy.20.limit_ref), custom_call_target="tpu_custom_call" | custom-call | flops 134217728 | bytes 1048576 | tf_op jit(solution)/shard_map/rows_attention/pallas_call | solution.py:210
  54.0 12.7 %all_to_all.26.parts_ref = bf16[8,16,384]{2,1,0:T(8,128)(2,1)} all-to-all(bf16[8,16,384]{2,1,0:T(8,128)(2,1)} %rows_attention.1), channel_id=1, replica_groups=mesh['seq'=8,'head'=4,'ctx_0'=8,'ctx_1'=2] {'seq'}, dimensions={0} | all-to-all | bytes 196608 | tf_op jit(solution)/shard_map/all_to_all | solution.py:306
  66.7 2.5 %merge.1 = bf16[16,16,256]{2,1,0:T(8,128)(2,1)} custom-call(s32[3]{0:T(128)} %pad_add_fusion.at_ref, bf16[8,16,384]{2,1,0:T(8,128)(2,1)} %all_to_all.26.parts_ref, bf16[8,16,256]{2,1,0:T(8,128)(2,1)} %sum_queries.1.q_ref, bf16[256,256]{1,0:T(8,128)(2,1)} %k_ref.1, bf16[256,256]{1,0:T(8,128)(2,1)} %v_ref.1), custom_call_target="tpu_custom_call" | custom-call | flops 196608 | bytes 196608 | tf_op jit(solution)/shard_map/merge/pallas_call | solution.py:249
  69.2 12.1 %all_to_all.27 = bf16[16,16,256]{2,1,0:T(8,128)(2,1)S(1)} all-to-all(bf16[16,16,256]{2,1,0:T(8,128)(2,1)} %merge.1), channel_id=1, replica_groups=mesh['seq'=8,'head'=4,'ctx_0'=8,'ctx_1'=2] {'ctx_0','ctx_1'}, dimensions={0} | all-to-all | bytes 262144 | tf_op jit(solution)/shard_map/all_to_all | solution.py:308
  81.3 0.0 copy-done.2
  81.3 0.2 fusion
  81.5 22.9 %all_to_all.28 = bf16[32,8,512]{2,1,0:T(8,128)(2,1)S(1)} all-to-all(bf16[32,8,512]{2,1,0:T(8,128)(2,1)S(1)} %fusion), channel_id=1, replica_groups=mesh['seq'=8,'head'=4,'ctx_0'=8,'ctx_1'=2] {'seq','head'}, dimensions={0} | all-to-all | bytes 524288 | tf_op jit(solution)/shard_map/all_to_all | solution.py:313
  104.4 0.6 reduce_sum.12
  105.1 0.0 all-gather.3.cloned.1.call-done
  105.1 9.4 %prefill.1 = bf16[512,128]{1,0:T(8,128)(2,1)} custom-call(s32[4]{0:T(128)} %off_ref.1, s32[1]{0:T(128)} %bitcast.seq_ref, bf16[512,128]{1,0:T(8,128)(2,1)} %q_ref.1, bf16[8,2048,128]{2,1,0:T(8,128)(2,1)} %bitcast.24), custom_call_target="tpu_custom_call" | custom-call | flops 2147483648 | bytes 4194304 | tf_op jit(solution)/shard_map/prefill/pallas_call | solution.py:112
Async XLA Ops:
  7.2 3.3 %copy-start = (bf16[256,512]{1,0:T(8,128)(2,1)S(1)}, bf16[256,512]{1,0:T(8,128)(2,1)}, u32[]{:S(2)}) copy-start(bf16[256,512]{1,0:T(8,128)(2,1)} %param.19) | copy-start | bytes 786436
  7.2 74.1 %copy-start.2 = (bf16[1,256,512]{2,1,0:T(8,128)(2,1)S(1)}, bf16[1,256,512]{2,1,0:T(8,128)(2,1)}, u32[]{:S(2)}) copy-start(bf16[1,256,512]{2,1,0:T(8,128)(2,1)} %param.21) | copy-start | bytes 786436
  7.2 97.9 %all-gather.3.cloned.1.call-start = ((), (), s32[]{:S(2)}) async-start(), calls=%async_computation.5 | async-start | bytes 4718592 | tf_op jit(solution)/shard_map/all_gather | solution.py:295
  31.9 18.7 %all-to-all-start.1 = ((bf16[8,16,256]{2,1,0:T(8,128)(2,1)}), bf16[8,16,256]{2,1,0:T(8,128)(2,1)S(1)}, u32[]{:S(2)}, u32[]{:S(2)}) async-start(bf16[8,16,256]{2,1,0:T(8,128)(2,1)} %sum_queries.1.q_ref), calls=%async_computation.1 | async-start | bytes 131072 | tf_op jit(solution)/shard_map/all_to_all | solution.py:302
  50.6 0.6 copy-start.1
Sparse Core Ops, SparseCore 0:
  10.6 66.9 all-gather.2
